TPU v7x, 256 devices: a whole 4x4x8 slice. The times are simulated.
256 devices in a mesh: snap: 4 (over z_hi), param: 64 (over z_lo, x, y, core).
Axes of the slice: x: 4, y: 4, z: 8 (z_hi: 4, z_lo: 2; z = z_hi * 2 + z_lo), core: 2. Of those that a mesh axis runs over, the one named last changes fastest.
Arguments:
- snapshots: bfloat16 [256, 4096, 1024], P('snap', 'param'), as said below
- coeffs: float32 [16, 256], P(None, 'snap'), may hold values from -0.375 to 0.375
Outputs:
- averages: float32 [16, 4096, 1024], P(None, 'param', 'snap')
- width_norms: float32 [16], replicated
Inputs may be any that keep to these rules, and one draw needn't show every extreme that they name: `snapshots`: stored snapshot weights, finite.
All inputs are finite; a program needn't handle non-finite values.
Results may differ from a plain program's by a relative error of at most 0.0003.
Values may be sent and summed in bfloat16 or wider, within the bound.
No kernel may reach another device: no remote copies, remote signals or barrier semaphores. Data moves between devices by JAX's collectives and lax.ppermute only.
A program may use at most 64 MiB of HBM per device.

v0:
```python
import functools

import jax
import jax.numpy as jnp
from jax import lax
from jax.experimental import pallas as pl
from jax.experimental.pallas import tpu as pltpu
from jax.sharding import PartitionSpec as P


GROUP = 8
BLOCK = 16
FLIGHT = 2
HALF = 128
CHUNK = 256
PARTS = (32, 32)

SPAN = 250.0
LN2 = 0.6931471805599453
PRE = 2.0**-8


def column_scale(values):
    top = jnp.max(jnp.abs(values), axis=0, keepdims=True)
    scale = jnp.clip(top * 1.0079, 2.0**-116, 3.38e38)
    return scale.astype(jnp.bfloat16).astype(jnp.float32)


def encode(values, scale):
    inverse = (SPAN * LN2 * PRE) / (scale * PRE)
    code = jnp.exp(jnp.abs(values) * inverse - (SPAN / 2 * LN2))
    return jnp.where(values < 0, -code, code).astype(jnp.bfloat16)


def decode(code, scale):
    code = code.astype(jnp.float32)
    level = jnp.log(jnp.abs(code)) + (SPAN / 2 * LN2)
    return jnp.where(code < 0, -level, level) * (scale * (1.0 / (SPAN * LN2)))


def fill_wide(c_ref, cbuf, sem, wide):
    widths, snaps = c_ref.shape
    depth = snaps * GROUP
    pltpu.make_async_copy(c_ref, cbuf, sem).wait()
    coeffs = cbuf[...]
    high = coeffs.astype(jnp.bfloat16)
    low = (coeffs - high.astype(jnp.float32)).astype(jnp.bfloat16)
    spread = (
        lax.shift_right_logical(lax.broadcasted_iota(jnp.int32, (snaps, depth), 1), 3)
        == lax.broadcasted_iota(jnp.int32, (snaps, depth), 0)
    ).astype(jnp.float32).astype(jnp.bfloat16)
    keep = (lax.broadcasted_iota(jnp.int32, (GROUP, depth), 1) & (GROUP - 1)) == lax.broadcasted_iota(
        jnp.int32, (GROUP, depth), 0
    )
    for part, piece in enumerate((high, low)):
        across = jnp.dot(piece, spread, preferred_element_type=jnp.float32)
        for w in range(widths):
            row = (part * widths + w) * GROUP
            wide[row : row + GROUP, :] = jnp.where(keep, across[w : w + 1, :], 0.0).astype(jnp.bfloat16)


def half_of(offset):
    return pl.multiple_of(lax.rem(2 * lax.axis_index("snap") + offset, 8) * HALF, HALF)


def multiply(x_ref, wide, start, offsets):
    depth = wide.shape[1]
    half = wide.shape[0] // 2
    halves = [x_ref[:, start : start + GROUP, pl.ds(half_of(offset), HALF)].reshape(depth, HALF) for offset in offsets]
    both = jnp.dot(wide[...], jnp.concatenate(halves, axis=1), preferred_element_type=jnp.float32)
    return (both[:half] + both[half:]).reshape(half // GROUP, GROUP, CHUNK)


def sent_kernel(start, rows, first, x_ref, c_ref, *refs):
    if first:
        up_ref, down_ref, x_out, wide, cbuf, csem, hold, scales, sems = refs
        pltpu.make_async_copy(c_ref, cbuf, csem).start()
    else:
        wide = c_ref
        up_ref, down_ref, x_out, hold, scales, sems = refs
    widths = wide.shape[0] // (2 * GROUP)
    blocks = rows // BLOCK
    copies = [
        pltpu.make_async_copy(
            x_ref.at[:, pl.ds(start + block * BLOCK, BLOCK), :],
            x_out.at[:, pl.ds(block * BLOCK, BLOCK), :],
            sems.at[block],
        )
        for block in range(blocks)
    ]
    for copy in copies[:FLIGHT]:
        copy.start()
    if first:
        fill_wide(c_ref, cbuf, csem, wide)
    for block in range(blocks):
        copies[block].wait()
        if block + FLIGHT < blocks:
            copies[block + FLIGHT].start()
        for at in range(block * BLOCK, (block + 1) * BLOCK, GROUP):
            hold[:, at : at + GROUP, :CHUNK] = multiply(x_out, wide, at, (4, 3))
            hold[:, at : at + GROUP, CHUNK:] = multiply(x_out, wide, at, (5, 6))
    for w in range(widths):
        value = hold[w]
        scale = column_scale(value)
        scales[w : w + 1, :] = scale
        code = encode(value, scale)
        up_ref[w * rows : (w + 1) * rows, :] = code[:, :CHUNK]
        down_ref[w * rows : (w + 1) * rows, :] = code[:, CHUNK:]
    packed = scales[...].astype(jnp.bfloat16)
    up_ref[widths * rows :, :] = packed[:, :CHUNK]
    down_ref[widths * rows :, :] = packed[:, CHUNK:]


def kept_kernel(wide, *refs):
    x_refs, (own_ref, fwd_up_ref, fwd_down_ref) = refs[:-3], refs[-3:]
    start = 0
    for x_ref in x_refs:
        for at in range(0, x_ref.shape[1], GROUP):
            r = slice(start + at, start + at + GROUP)
            own_ref[:, r, :] = multiply(x_ref, wide, at, (0, 1))
            value = multiply(x_ref, wide, at, (2, 7))
            fwd_up_ref[:, r, :] = value[:, :, :HALF]
            fwd_down_ref[:, r, :] = value[:, :, HALF:]
        start += x_ref.shape[1]


def relay_kernel(start, rows, prev_ref, next_ref, own_ref, fwd_up_ref, fwd_down_ref, up_ref, down_ref, sum_ref, scales):
    widths = own_ref.shape[0]
    t = slice(start, start + rows)
    prev_scale = prev_ref[widths * rows :, :].astype(jnp.float32)
    next_scale = next_ref[widths * rows :, :].astype(jnp.float32)
    for w in range(widths):
        r = slice(w * rows, (w + 1) * rows)
        got_prev = decode(prev_ref[r, :], prev_scale[w : w + 1, :])
        got_next = decode(next_ref[r, :], next_scale[w : w + 1, :])
        up = fwd_up_ref[w, t, :] + got_prev[:, :HALF]
        down = fwd_down_ref[w, t, :] + got_next[:, :HALF]
        up_scale = column_scale(up)
        down_scale = column_scale(down)
        scales[w : w + 1, :HALF] = up_scale
        scales[w : w + 1, HALF:] = down_scale
        up_ref[r, :] = encode(up, up_scale)
        down_ref[r, :] = encode(down, down_scale)
        sum_ref[w, :, :HALF] = own_ref[w, t, :HALF] + got_next[:, HALF:]
        sum_ref[w, :, HALF:] = own_ref[w, t, HALF:] + got_prev[:, HALF:]
    packed = scales[...].astype(jnp.bfloat16)
    up_ref[widths * rows :, :] = packed[:, :HALF]
    down_ref[widths * rows :, :] = packed[:, HALF:]


def final_kernel(start, rows, first, last, prev_ref, next_ref, sum_ref, *refs):
    refs = list(refs)
    before_ref = None if first else refs.pop(0)
    if not first:
        refs.pop(0)
    out_ref, squares_ref, block, total, sem = refs
    widths = sum_ref.shape[0]
    prev_scale = prev_ref[widths * rows :, :].astype(jnp.float32)
    next_scale = next_ref[widths * rows :, :].astype(jnp.float32)
    for w in range(widths):
        r = slice(w * rows, (w + 1) * rows)
        left = sum_ref[w, :, :HALF] + decode(prev_ref[r, :], prev_scale[w : w + 1, :])
        right = sum_ref[w, :, HALF:] + decode(next_ref[r, :], next_scale[w : w + 1, :])
        block[w, :, :HALF] = left
        block[w, :, HALF:] = right
        total[w : w + 1, :] = jnp.sum(left * left + right * right, axis=0, keepdims=True)
    copy = pltpu.make_async_copy(block, out_ref.at[:, pl.ds(start, rows), :], sem)
    copy.start()
    squares = total[...] if first else total[...] + before_ref[...]
    if last:
        squares = lax.dot_general(
            jnp.ones((squares_ref.shape[0], HALF), jnp.float32),
            squares,
            (((1,), (1,)), ((), ())),
            precision=lax.Precision.HIGHEST,
            preferred_element_type=jnp.float32,
        )
    squares_ref[...] = squares
    copy.wait()


def vmem():
    return pl.BlockSpec(memory_space=pltpu.VMEM)


def hbm():
    return pl.BlockSpec(memory_space=pl.ANY)


def held(array):
    return pltpu.with_memory_space_constraint(array, pltpu.VMEM)


def placed(array):
    return pltpu.with_memory_space_constraint(array, pltpu.HBM)


def cost(flops):
    return pl.CostEstimate(flops=flops, bytes_accessed=2_000_000, transcendentals=0)


def params(mib):
    return pltpu.CompilerParams(vmem_limit_bytes=mib * 2**20)


def sent_sums(snapshots, start, rows, coeffs=None, wide=None):
    first = wide is None
    snaps, _, columns = snapshots.shape
    widths = coeffs.shape[0] if first else wide.shape[0] // (2 * GROUP)
    tall = widths * rows + widths
    wide_shape = pltpu.VMEM((2 * widths * GROUP, snaps * GROUP), jnp.bfloat16)
    return pl.pallas_call(
        functools.partial(sent_kernel, start, rows, first),
        in_specs=[hbm(), hbm() if first else vmem()],
        out_specs=[vmem()] * (4 if first else 3),
        out_shape=[pltpu.VMEM((tall, CHUNK), jnp.bfloat16)] * 2
        + [pltpu.VMEM((snaps, rows, columns), jnp.bfloat16)]
        + [wide_shape] * first,
        scratch_shapes=[pltpu.VMEM((widths, snaps), jnp.float32), pltpu.SemaphoreType.DMA] * first
        + [
            pltpu.VMEM((widths, rows, 2 * CHUNK), jnp.float32),
            pltpu.VMEM((widths, 2 * CHUNK), jnp.float32),
            pltpu.SemaphoreType.DMA((rows // BLOCK,)),
        ],
        cost_estimate=cost(4_000_000_000),
        compiler_params=params(14),
        name="sent_sums",
    )(placed(snapshots), placed(coeffs) if first else held(wide))


def kept_sums(wide, parts):
    widths = wide.shape[0] // (2 * GROUP)
    rows = sum(part.shape[1] for part in parts)
    return pl.pallas_call(
        kept_kernel,
        in_specs=[vmem()] * (1 + len(parts)),
        out_specs=[vmem()] * 3,
        out_shape=[
            pltpu.VMEM((widths, rows, CHUNK), jnp.float32),
            pltpu.VMEM((widths, rows, HALF), jnp.float32),
            pltpu.VMEM((widths, rows, HALF), jnp.float32),
        ],
        cost_estimate=cost(6_000_000_000),
        compiler_params=params(16),
        name="kept_sums",
    )(held(wide), *[held(part) for part in parts])


def relay(start, rows, got_prev, got_next, own, fwd_up, fwd_down):
    widths = own.shape[0]
    tall = widths * rows + widths
    return pl.pallas_call(
        functools.partial(relay_kernel, start, rows),
        in_specs=[vmem()] * 5,
        out_specs=[vmem()] * 3,
        out_shape=[
            pltpu.VMEM((tall, HALF), jnp.bfloat16),
            pltpu.VMEM((tall, HALF), jnp.bfloat16),
            pltpu.VMEM((widths, rows, CHUNK), jnp.float32),
        ],
        scratch_shapes=[pltpu.VMEM((widths, CHUNK), jnp.float32)],
        cost_estimate=cost(2_000_000_000),
        compiler_params=params(4),
        name="relay",
    )(held(got_prev), held(got_next), held(own), held(fwd_up), held(fwd_down))


def finish(start, rows, total_rows, devices, last, got_prev, got_next, summed, squares, averages):
    widths = summed.shape[0]
    first = averages is None
    operands = [held(got_prev), held(got_next), held(summed)]
    specs = [vmem()] * 3
    if not first:
        operands += [held(squares), averages]
        specs += [vmem(), hbm()]
    return pl.pallas_call(
        functools.partial(final_kernel, start, rows, first, last),
        in_specs=specs,
        out_specs=[hbm(), vmem()],
        out_shape=[
            jax.ShapeDtypeStruct((widths, total_rows, CHUNK), jnp.float32),
            pltpu.VMEM((devices, widths) if last else (widths, HALF), jnp.float32),
        ],
        input_output_aliases={} if first else {4: 0},
        scratch_shapes=[
            pltpu.VMEM((widths, rows, CHUNK), jnp.float32),
            pltpu.VMEM((widths, HALF), jnp.float32),
            pltpu.SemaphoreType.DMA,
        ],
        cost_estimate=cost(1_000_000_000),
        compiler_params=params(4),
        name="finish",
    )(*operands)


def on_device(snapshots, coeffs):
    axes = ("snap", "param")
    groups = lax.axis_size("snap")
    devices = lax.axis_size(axes)
    total_rows = snapshots.shape[1]
    up_pairs = [(i, (i + 1) % groups) for i in range(groups)]
    down_pairs = [(i, (i - 1) % groups) for i in range(groups)]

    starts = [sum(PARTS[:k]) for k in range(len(PARTS))]

    def both_ways(up, down):
        up = lax.ppermute(up, "snap", up_pairs)
        down = lax.ppermute(down, "snap", down_pairs)
        return up, down

    first, parts, wide = [], [], None
    for start, rows in zip(starts, PARTS):
        up, down, part, *made = sent_sums(snapshots, start, rows, coeffs, wide)
        parts.append(part)
        wide = made[0] if made else wide
        first.append(both_ways(up, down))
    kept = kept_sums(wide, parts)
    second = []
    for start, rows, got in zip(starts, PARTS, first):
        up, down, summed = relay(start, rows, *got, *kept)
        second.append((*both_ways(up, down), summed))
    averages = squares = None
    for start, rows, got in zip(starts, PARTS, second):
        last = start + rows == total_rows
        averages, squares = finish(start, rows, total_rows, devices, last, *got, squares, averages)
    theirs = lax.all_to_all(squares, axes, 0, 0, tiled=True)
    entries = averages.shape[1] * averages.shape[2] * devices
    width_norms = jnp.sqrt(jnp.sum(theirs, axis=0) / jnp.float32(entries))
    return (averages, width_norms)


def solution(mesh):
    return jax.shard_map(
        on_device,
        mesh=mesh,
        in_specs=(P("snap", "param", None), P(None, "snap")),
        out_specs=(P(None, "param", "snap"), P()),
        check_vma=False,
    )
```

profile of v0, /device:TPU:1, one launch (start us, length us, event | category | flops | bytes accessed | tf_op | source)
XLA Modules:
  0.0 75.2 jit_solution(12455821286819947780)
XLA Ops:
  0.6 3.3 %sent_sums.2 = (bf16[528,256]{1,0:T(8,128)(2,1)S(1)}, bf16[528,256]{1,0:T(8,128)(2,1)S(1)}, bf16[64,32,1024]{2,1,0:T(8,128)(2,1)S(1)}, bf16[256,512]{1,0:T(8,128)(2,1)S(1)}) custom-call(bf16[64,64,1024]{2,1,0:T(8,128)(2,1)} %x_ref.3, f32[16,64]{1,0:T(8,128)} %c_ref.1), custom_call_target="tpu_custom_call" | custom-call | flops 4000000000 | bytes 2000000 | tf_op jit(solution)/shard_map/sent_sums/pallas_call | solution.py:212
  3.9 3.9 %collective-permute-start.4 = (bf16[528,256]{1,0:T(8,128)(2,1)S(1)}, bf16[528,256]{1,0:T(8,128)(2,1)S(1)}, u32[]{:S(2)}, u32[]{:S(2)}) collective-permute-start(bf16[528,256]{1,0:T(8,128)(2,1)S(1)} %get-tuple-element.33), channel_id=1, source_target_pairs={{0,64},{64,128},{128,192},{192,0},{1,65},{65,129},{129,193},{193,1... | collective-permute-start | bytes 811016 | tf_op jit(solution)/shard_map/ppermute | solution.py:307
  7.8 3.1 %collective-permute-start.5 = (bf16[528,256]{1,0:T(8,128)(2,1)S(1)}, bf16[528,256]{1,0:T(8,128)(2,1)S(1)}, u32[]{:S(2)}, u32[]{:S(2)}) collective-permute-start(bf16[528,256]{1,0:T(8,128)(2,1)S(1)} %get-tuple-element.34), channel_id=1, source_target_pairs={{0,192},{64,0},{128,64},{192,128},{1,193},{65,1},{129,65},{193,129... | collective-permute-start | bytes 811016 | tf_op jit(solution)/shard_map/ppermute | solution.py:308
  10.9 3.2 %sent_sums.3 = (bf16[528,256]{1,0:T(8,128)(2,1)S(1)}, bf16[528,256]{1,0:T(8,128)(2,1)S(1)}, bf16[64,32,1024]{2,1,0:T(8,128)(2,1)S(1)}) custom-call(bf16[64,64,1024]{2,1,0:T(8,128)(2,1)} %x_ref.3, bf16[256,512]{1,0:T(8,128)(2,1)S(1)} %get-tuple-element.22.c_ref.wide), custom_call_target="tpu_custom_call" | custom-call | flops 4000000000 | bytes 2000000 | tf_op jit(solution)/shard_map/sent_sums/pallas_call | solution.py:212
  14.2 1.2 %collective-permute-start = (bf16[528,256]{1,0:T(8,128)(2,1)S(1)}, bf16[528,256]{1,0:T(8,128)(2,1)S(1)}, u32[]{:S(2)}, u32[]{:S(2)}) collective-permute-start(bf16[528,256]{1,0:T(8,128)(2,1)S(1)} %get-tuple-element.23), channel_id=1, source_target_pairs={{0,64},{64,128},{128,192},{192,0},{1,65},{65,129},{129,193},{193,1... | collective-permute-start | bytes 811016 | tf_op jit(solution)/shard_map/ppermute | solution.py:307
  15.3 2.5 %collective-permute-start.1 = (bf16[528,256]{1,0:T(8,128)(2,1)S(1)}, bf16[528,256]{1,0:T(8,128)(2,1)S(1)}, u32[]{:S(2)}, u32[]{:S(2)}) collective-permute-start(bf16[528,256]{1,0:T(8,128)(2,1)S(1)} %get-tuple-element.24), channel_id=1, source_target_pairs={{0,192},{64,0},{128,64},{192,128},{1,193},{65,1},{129,65},{193,129... | collective-permute-start | bytes 811016 | tf_op jit(solution)/shard_map/ppermute | solution.py:308
  17.8 1.5 %kept_sums.1 = (f32[16,64,256]{2,1,0:T(8,128)S(1)}, f32[16,64,128]{2,1,0:T(8,128)S(1)}, f32[16,64,128]{2,1,0:T(8,128)S(1)}) custom-call(bf16[256,512]{1,0:T(8,128)(2,1)S(1)} %get-tuple-element.22.c_ref.wide, bf16[64,32,1024]{2,1,0:T(8,128)(2,1)S(1)} %get-tuple-element.25.refs_0_, bf16[64,32,1024]{2,1,0:T(8,128)(2,1)S(1)} %get-tuple-element.26.refs_1_), custom_call_target="tpu_custom_call" | custom-call | flops 6000000000 | bytes 2000000 | tf_op jit(solution)/shard_map/kept_sums/pallas_call | solution.py:234
  19.4 0.0 collective-permute-done.4.prev_ref
  19.4 10.7 %collective-permute-done.5.next_ref = bf16[528,256]{1,0:T(8,128)(2,1)S(1)} collective-permute-done((bf16[528,256]{1,0:T(8,128)(2,1)S(1)}, bf16[528,256]{1,0:T(8,128)(2,1)S(1)}, u32[]{:S(2)}, u32[]{:S(2)}) %collective-permute-start.5) | collective-permute-done | bytes 270368 | tf_op jit(solution)/shard_map/ppermute | solution.py:308
  30.1 0.6 relay.3
  30.7 3.2 %collective-permute-start.6 = (bf16[528,128]{1,0:T(8,128)(2,1)S(1)}, bf16[528,128]{1,0:T(8,128)(2,1)S(1)}, u32[]{:S(2)}, u32[]{:S(2)}) collective-permute-start(bf16[528,128]{1,0:T(8,128)(2,1)S(1)} %get-tuple-element.35), channel_id=1, source_target_pairs={{0,64},{64,128},{128,192},{192,0},{1,65},{65,129},{129,193},{193,1... | collective-permute-start | bytes 405512 | tf_op jit(solution)/shard_map/ppermute | solution.py:307
  33.9 0.5 collective-permute-start.7
  34.3 0.0 collective-permute-done.prev_ref
  34.3 1.6 %collective-permute-done.1.next_ref = bf16[528,256]{1,0:T(8,128)(2,1)S(1)} collective-permute-done((bf16[528,256]{1,0:T(8,128)(2,1)S(1)}, bf16[528,256]{1,0:T(8,128)(2,1)S(1)}, u32[]{:S(2)}, u32[]{:S(2)}) %collective-permute-start.1) | collective-permute-done | bytes 270368 | tf_op jit(solution)/shard_map/ppermute | solution.py:308
  36.0 0.6 relay.2
  36.6 3.2 %collective-permute-start.2 = (bf16[528,128]{1,0:T(8,128)(2,1)S(1)}, bf16[528,128]{1,0:T(8,128)(2,1)S(1)}, u32[]{:S(2)}, u32[]{:S(2)}) collective-permute-start(bf16[528,128]{1,0:T(8,128)(2,1)S(1)} %get-tuple-element.30), channel_id=1, source_target_pairs={{0,64},{64,128},{128,192},{192,0},{1,65},{65,129},{129,193},{193,1... | collective-permute-start | bytes 405512 | tf_op jit(solution)/shard_map/ppermute | solution.py:307
  39.8 0.5 collective-permute-start.3
  40.2 3.1 %collective-permute-done.6.prev_ref = bf16[528,128]{1,0:T(8,128)(2,1)S(1)} collective-permute-done((bf16[528,128]{1,0:T(8,128)(2,1)S(1)}, bf16[528,128]{1,0:T(8,128)(2,1)S(1)}, u32[]{:S(2)}, u32[]{:S(2)}) %collective-permute-start.6) | collective-permute-done | bytes 135200 | tf_op jit(solution)/shard_map/ppermute | solution.py:307
  43.4 0.0 collective-permute-done.7.next_ref
  43.4 1.0 %finish.2 = (f32[16,64,256]{2,1,0:T(8,128)}, f32[16,128]{1,0:T(8,128)S(1)}) custom-call(bf16[528,128]{1,0:T(8,128)(2,1)S(1)} %collective-permute-done.6.prev_ref, bf16[528,128]{1,0:T(8,128)(2,1)S(1)} %collective-permute-done.7.next_ref, f32[16,32,256]{2,1,0:T(8,128)S(1)} %get-tuple-element.37.sum_ref), custom_call_target="tpu_custom_call" | custom-call | flops 1000000000 | bytes 2000000 | tf_op jit(solution)/shard_map/finish/pallas_call | solution.py:276
  44.4 3.7 %collective-permute-done.2.prev_ref = bf16[528,128]{1,0:T(8,128)(2,1)S(1)} collective-permute-done((bf16[528,128]{1,0:T(8,128)(2,1)S(1)}, bf16[528,128]{1,0:T(8,128)(2,1)S(1)}, u32[]{:S(2)}, u32[]{:S(2)}) %collective-permute-start.2) | collective-permute-done | bytes 135200 | tf_op jit(solution)/shard_map/ppermute | solution.py:307
  48.1 2.2 %collective-permute-done.3.next_ref = bf16[528,128]{1,0:T(8,128)(2,1)S(1)} collective-permute-done((bf16[528,128]{1,0:T(8,128)(2,1)S(1)}, bf16[528,128]{1,0:T(8,128)(2,1)S(1)}, u32[]{:S(2)}, u32[]{:S(2)}) %collective-permute-start.3) | collective-permute-done | bytes 135200 | tf_op jit(solution)/shard_map/ppermute | solution.py:308
  50.2 1.0 %finish.3 = (f32[16,64,256]{2,1,0:T(8,128)}, f32[256,16]{1,0:T(8,128)S(1)}) custom-call(bf16[528,128]{1,0:T(8,128)(2,1)S(1)} %collective-permute-done.2.prev_ref, bf16[528,128]{1,0:T(8,128)(2,1)S(1)} %collective-permute-done.3.next_ref, f32[16,32,256]{2,1,0:T(8,128)S(1)} %get-tuple-element.32.sum_ref, ...), custom_call_target="tpu_custom_call", output_to_operand_aliasing={{0}: (4, {})} | custom-call | flops 1000000000 | bytes 2000000 | tf_op jit(solution)/shard_map/finish/pallas_call | solution.py:276
  51.2 23.2 %all_to_all.9 = f32[256,1,16]{2,1,0:T(1,128)S(1)} all-to-all(f32[256,1,16]{2,1,0:T(1,128)S(1)} %bitcast.3), channel_id=1, replica_groups=mesh['snap'=4,'param'=64] {'snap','param'}, dimensions={0} | all-to-all | bytes 32768 | tf_op jit(solution)/shard_map/all_to_all | solution.py:326
  74.4 0.3 reduce_sum.9
  74.7 0.5 multiply_sqrt_fusion
Async XLA Ops:
  3.9 15.4 %collective-permute-start.4 = (bf16[528,256]{1,0:T(8,128)(2,1)S(1)}, bf16[528,256]{1,0:T(8,128)(2,1)S(1)}, u32[]{:S(2)}, u32[]{:S(2)}) collective-permute-start(bf16[528,256]{1,0:T(8,128)(2,1)S(1)} %get-tuple-element.33), channel_id=1, source_target_pairs={{0,64},{64,128},{128,192},{192,0},{1,65},{65,129},{129,193},{193,1... | collective-permute-start | bytes 811016 | tf_op jit(solution)/shard_map/ppermute | solution.py:307
  7.8 22.3 %collective-permute-start.5 = (bf16[528,256]{1,0:T(8,128)(2,1)S(1)}, bf16[528,256]{1,0:T(8,128)(2,1)S(1)}, u32[]{:S(2)}, u32[]{:S(2)}) collective-permute-start(bf16[528,256]{1,0:T(8,128)(2,1)S(1)} %get-tuple-element.34), channel_id=1, source_target_pairs={{0,192},{64,0},{128,64},{192,128},{1,193},{65,1},{129,65},{193,129... | collective-permute-start | bytes 811016 | tf_op jit(solution)/shard_map/ppermute | solution.py:308
  14.2 20.2 %collective-permute-start = (bf16[528,256]{1,0:T(8,128)(2,1)S(1)}, bf16[528,256]{1,0:T(8,128)(2,1)S(1)}, u32[]{:S(2)}, u32[]{:S(2)}) collective-permute-start(bf16[528,256]{1,0:T(8,128)(2,1)S(1)} %get-tuple-element.23), channel_id=1, source_target_pairs={{0,64},{64,128},{128,192},{192,0},{1,65},{65,129},{129,193},{193,1... | collective-permute-start | bytes 811016 | tf_op jit(solution)/shard_map/ppermute | solution.py:307
  15.3 20.6 %collective-permute-start.1 = (bf16[528,256]{1,0:T(8,128)(2,1)S(1)}, bf16[528,256]{1,0:T(8,128)(2,1)S(1)}, u32[]{:S(2)}, u32[]{:S(2)}) collective-permute-start(bf16[528,256]{1,0:T(8,128)(2,1)S(1)} %get-tuple-element.24), channel_id=1, source_target_pairs={{0,192},{64,0},{128,64},{192,128},{1,193},{65,1},{129,65},{193,129... | collective-permute-start | bytes 811016 | tf_op jit(solution)/shard_map/ppermute | solution.py:308
  30.7 12.7 %collective-permute-start.6 = (bf16[528,128]{1,0:T(8,128)(2,1)S(1)}, bf16[528,128]{1,0:T(8,128)(2,1)S(1)}, u32[]{:S(2)}, u32[]{:S(2)}) collective-permute-start(bf16[528,128]{1,0:T(8,128)(2,1)S(1)} %get-tuple-element.35), channel_id=1, source_target_pairs={{0,64},{64,128},{128,192},{192,0},{1,65},{65,129},{129,193},{193,1... | collective-permute-start | bytes 405512 | tf_op jit(solution)/shard_map/ppermute | solution.py:307
  33.9 9.5 %collective-permute-start.7 = (bf16[528,128]{1,0:T(8,128)(2,1)S(1)}, bf16[528,128]{1,0:T(8,128)(2,1)S(1)}, u32[]{:S(2)}, u32[]{:S(2)}) collective-permute-start(bf16[528,128]{1,0:T(8,128)(2,1)S(1)} %get-tuple-element.36), channel_id=1, source_target_pairs={{0,192},{64,0},{128,64},{192,128},{1,193},{65,1},{129,65},{193,129... | collective-permute-start | bytes 405512 | tf_op jit(solution)/shard_map/ppermute | solution.py:308
  36.6 11.5 %collective-permute-start.2 = (bf16[528,128]{1,0:T(8,128)(2,1)S(1)}, bf16[528,128]{1,0:T(8,128)(2,1)S(1)}, u32[]{:S(2)}, u32[]{:S(2)}) collective-permute-start(bf16[528,128]{1,0:T(8,128)(2,1)S(1)} %get-tuple-element.30), channel_id=1, source_target_pairs={{0,64},{64,128},{128,192},{192,0},{1,65},{65,129},{129,193},{193,1... | collective-permute-start | bytes 405512 | tf_op jit(solution)/shard_map/ppermute | solution.py:307
  39.8 10.5 %collective-permute-start.3 = (bf16[528,128]{1,0:T(8,128)(2,1)S(1)}, bf16[528,128]{1,0:T(8,128)(2,1)S(1)}, u32[]{:S(2)}, u32[]{:S(2)}) collective-permute-start(bf16[528,128]{1,0:T(8,128)(2,1)S(1)} %get-tuple-element.31), channel_id=1, source_target_pairs={{0,192},{64,0},{128,64},{192,128},{1,193},{65,1},{129,65},{193,129... | collective-permute-start | bytes 405512 | tf_op jit(solution)/shard_map/ppermute | solution.py:308
where the time goes:
time: 75.3 us; the launch traced here: 75.2 us
  blocking collectives  23.2 us (31%)
  waiting for transfers between devices  21.3 us (28%)
  starting transfers between devices  18 us (24%)
  Pallas kernels  11.3 us (15%)
  other arithmetic  0.81 us (1%)
    all_to_all x1, blocking collectives, on_device(): theirs = lax.all_to_all(squares, axes, 0, 0, tiled=True)  23.2 us
    ppermute x4, waiting for transfers between devices, both_ways(): down = lax.ppermute(down, 'snap', down_pairs)  14.5 us
    ppermute x4, starting transfers between devices, both_ways(): up = lax.ppermute(up, 'snap', up_pairs)  11.4 us
    ppermute x4, waiting for transfers between devices, both_ways(): up = lax.ppermute(up, 'snap', up_pairs)  6.8 us
    ppermute x4, starting transfers between devices, both_ways(): down = lax.ppermute(down, 'snap', down_pairs)  6.54 us
    pallas_call x2, Pallas kernels, sent_sums(): pl.pallas_call(functools.partial(sent_kernel, start, rows, first), in_spe...  6.53 us
    pallas_call x2, Pallas kernels, finish(): pl.pallas_call(functools.partial(final_kernel, start, rows, first, last),...  2.05 us
    pallas_call x1, Pallas kernels, kept_sums(): pl.pallas_call(kept_kernel, in_specs=[vmem()] * (1 + len(parts)), out_spe...  1.52 us
  transfers between devices with their start and end apart: 8, of which 5 were waited for; matrix products, arithmetic and copies ran while one was open for 0% of the time, Pallas kernels for 9%

commit v1 on v0

--- a/solution.py
+++ b/solution.py
@@ -13,7 +13,7 @@
 FLIGHT = 2
 HALF = 128
 CHUNK = 256
-PARTS = (32, 32)
+PARTS = (16, 32, 16)
 
 SPAN = 250.0
 LN2 = 0.6931471805599453
@@ -57,6 +57,10 @@
         for w in range(widths):
             row = (part * widths + w) * GROUP
             wide[row : row + GROUP, :] = jnp.where(keep, across[w : w + 1, :], 0.0).astype(jnp.bfloat16)
+
+
+def side():
+    return lax.rem(lax.axis_index("snap"), 2)
 
 
 def half_of(offset):
@@ -92,13 +96,14 @@
         copy.start()
     if first:
         fill_wide(c_ref, cbuf, csem, wide)
+    p = side() if first else 0
     for block in range(blocks):
         copies[block].wait()
         if block + FLIGHT < blocks:
             copies[block + FLIGHT].start()
         for at in range(block * BLOCK, (block + 1) * BLOCK, GROUP):
-            hold[:, at : at + GROUP, :CHUNK] = multiply(x_out, wide, at, (4, 3))
-            hold[:, at : at + GROUP, CHUNK:] = multiply(x_out, wide, at, (5, 6))
+            hold[:, at : at + GROUP, :CHUNK] = multiply(x_out, wide, at, (4 + p, 3 + 3 * p))
+            hold[:, at : at + GROUP, CHUNK:] = multiply(x_out, wide, at, (5 - p, 6 - 3 * p))
     for w in range(widths):
         value = hold[w]
         scale = column_scale(value)
@@ -124,15 +129,18 @@
         start += x_ref.shape[1]
 
 
-def relay_kernel(start, rows, prev_ref, next_ref, own_ref, fwd_up_ref, fwd_down_ref, up_ref, down_ref, sum_ref, scales):
+def relay_kernel(start, rows, pairwise, prev_ref, next_ref, own_ref, fwd_up_ref, fwd_down_ref, up_ref, down_ref, sum_ref, scales):
     widths = own_ref.shape[0]
     t = slice(start, start + rows)
+    swap = side() == 0
     prev_scale = prev_ref[widths * rows :, :].astype(jnp.float32)
     next_scale = next_ref[widths * rows :, :].astype(jnp.float32)
     for w in range(widths):
         r = slice(w * rows, (w + 1) * rows)
         got_prev = decode(prev_ref[r, :], prev_scale[w : w + 1, :])
         got_next = decode(next_ref[r, :], next_scale[w : w + 1, :])
+        if pairwise:
+            got_prev, got_next = jnp.where(swap, got_next, got_prev), jnp.where(swap, got_prev, got_next)
         up = fwd_up_ref[w, t, :] + got_prev[:, :HALF]
         down = fwd_down_ref[w, t, :] + got_next[:, :HALF]
         up_scale = column_scale(up)
@@ -250,7 +258,7 @@
     widths = own.shape[0]
     tall = widths * rows + widths
     return pl.pallas_call(
-        functools.partial(relay_kernel, start, rows),
+        functools.partial(relay_kernel, start, rows, start == 0),
         in_specs=[vmem()] * 5,
         out_specs=[vmem()] * 3,
         out_shape=[
@@ -301,19 +309,23 @@
     up_pairs = [(i, (i + 1) % groups) for i in range(groups)]
     down_pairs = [(i, (i - 1) % groups) for i in range(groups)]
 
+    pairs = (
+        [(i, (i + 1 - 2 * (i % 2)) % groups) for i in range(groups)],
+        [(i, (i - 1 + 2 * (i % 2)) % groups) for i in range(groups)],
+    )
     starts = [sum(PARTS[:k]) for k in range(len(PARTS))]
 
-    def both_ways(up, down):
+    def both_ways(up, down, up_pairs=up_pairs, down_pairs=down_pairs):
         up = lax.ppermute(up, "snap", up_pairs)
         down = lax.ppermute(down, "snap", down_pairs)
         return up, down
 
     first, parts, wide = [], [], None
-    for start, rows in zip(starts, PARTS):
+    for k, (start, rows) in enumerate(zip(starts, PARTS)):
         up, down, part, *made = sent_sums(snapshots, start, rows, coeffs, wide)
         parts.append(part)
         wide = made[0] if made else wide
-        first.append(both_ways(up, down))
+        first.append(both_ways(up, down, *(pairs if k == 0 else ())))
     kept = kept_sums(wide, parts)
     second = []
     for start, rows, got in zip(starts, PARTS, first):

time: 75.3 us -> 78.3 us (1.040)
  waiting for transfers between devices: 21.3 us -> 12.6 us
  starting transfers between devices: 18 us -> 24.3 us
  blocking collectives: 23.2 us -> 26 us
  Pallas kernels: 11.3 us -> 13.6 us
    ppermute x4 -> x6, waiting for transfers between devices: 14.5 us -> 1.68 us  [both_ways(): down = lax.ppermute(down, 'snap', down_pairs)]
    ppermute x4 -> x6, starting transfers between devices: 6.54 us -> 15.9 us  [both_ways(): down = lax.ppermute(down, 'snap', down_pairs)]
    ppermute x4 -> x6, waiting for transfers between devices: 6.8 us -> 11 us  [both_ways(): up = lax.ppermute(up, 'snap', up_pairs)]
    ppermute x4 -> x6, starting transfers between devices: 11.4 us -> 8.41 us  [both_ways(): up = lax.ppermute(up, 'snap', up_pairs)]
    all_to_all x1, blocking collectives: 23.2 us -> 26 us  [on_device(): theirs = lax.all_to_all(squares, axes, 0, 0, tiled=True)]
    pallas_call x2 -> x3, Pallas kernels: 6.53 us -> 8.11 us  [sent_sums(): pl.pallas_call(functools.partial(sent_kernel, start, rows, first), in_spe...]
    pallas_call x2 -> x3, Pallas kernels: 2.05 us -> 2.69 us  [finish(): pl.pallas_call(functools.partial(final_kernel, start, rows, first, last),...]
  transfers between devices with their start and end apart: 8 -> 12, of which waited for: 5 -> 3; matrix products, arithmetic and copies ran while one was open for 0% -> 0% of each run, Pallas kernels for 9% -> 13%
where the time goes in v1:
time: 78.3 us; the launch traced here: 78.2 us
  blocking collectives  26 us (33%)
  starting transfers between devices  24.3 us (31%)
  Pallas kernels  13.6 us (17%)
  waiting for transfers between devices  12.6 us (16%)
  other arithmetic  0.81 us (1%)
    all_to_all x1, blocking collectives, on_device(): theirs = lax.all_to_all(squares, axes, 0, 0, tiled=True)  26 us
    ppermute x6, starting transfers between devices, both_ways(): down = lax.ppermute(down, 'snap', down_pairs)  15.9 us
    ppermute x6, waiting for transfers between devices, both_ways(): up = lax.ppermute(up, 'snap', up_pairs)  11 us
    ppermute x6, starting transfers between devices, both_ways(): up = lax.ppermute(up, 'snap', up_pairs)  8.41 us
    pallas_call x3, Pallas kernels, sent_sums(): pl.pallas_call(functools.partial(sent_kernel, start, rows, first), in_spe...  8.11 us
    pallas_call x3, Pallas kernels, finish(): pl.pallas_call(functools.partial(final_kernel, start, rows, first, last),...  2.69 us
    ppermute x6, waiting for transfers between devices, both_ways(): down = lax.ppermute(down, 'snap', down_pairs)  1.68 us
  transfers between devices with their start and end apart: 12, of which 3 were waited for; matrix products, arithmetic and copies ran while one was open for 0% of the time, Pallas kernels for 13%

profile of v1, /device:TPU:1, one launch (start us, length us, event | category | flops | bytes accessed | tf_op | source)
XLA Modules:
  0.0 78.2 jit_solution(11789474171027361155)
XLA Ops:
  0.6 2.4 %sent_sums.3 = (bf16[272,256]{1,0:T(8,128)(2,1)S(1)}, bf16[272,256]{1,0:T(8,128)(2,1)S(1)}, bf16[64,16,1024]{2,1,0:T(8,128)(2,1)S(1)}, bf16[256,512]{1,0:T(8,128)(2,1)S(1)}) custom-call(bf16[64,64,1024]{2,1,0:T(8,128)(2,1)} %x_ref.5, f32[16,64]{1,0:T(8,128)} %c_ref.1), custom_call_target="tpu_custom_call" | custom-call | flops 4000000000 | bytes 2000000 | tf_op jit(solution)/shard_map/sent_sums/pallas_call | solution.py:220
  3.1 3.9 %collective-permute-start.8 = (bf16[272,256]{1,0:T(8,128)(2,1)S(1)}, bf16[272,256]{1,0:T(8,128)(2,1)S(1)}, u32[]{:S(2)}, u32[]{:S(2)}) collective-permute-start(bf16[272,256]{1,0:T(8,128)(2,1)S(1)} %get-tuple-element.47), channel_id=1, source_target_pairs={{0,64},{64,0},{128,192},{192,128},{1,65},{65,1},{129,193},{193,129... | collective-permute-start | bytes 417800 | tf_op jit(solution)/shard_map/ppermute | solution.py:319
  7.0 4.2 %collective-permute-start.9 = (bf16[272,256]{1,0:T(8,128)(2,1)S(1)}, bf16[272,256]{1,0:T(8,128)(2,1)S(1)}, u32[]{:S(2)}, u32[]{:S(2)}) collective-permute-start(bf16[272,256]{1,0:T(8,128)(2,1)S(1)} %get-tuple-element.48), channel_id=1, source_target_pairs={{0,192},{64,128},{128,64},{192,0},{1,193},{65,129},{129,65},{193,1... | collective-permute-start | bytes 417800 | tf_op jit(solution)/shard_map/ppermute | solution.py:320
  11.2 2.4 %sent_sums.4 = (bf16[272,256]{1,0:T(8,128)(2,1)S(1)}, bf16[272,256]{1,0:T(8,128)(2,1)S(1)}, bf16[64,16,1024]{2,1,0:T(8,128)(2,1)S(1)}) custom-call(bf16[64,64,1024]{2,1,0:T(8,128)(2,1)} %x_ref.5, bf16[256,512]{1,0:T(8,128)(2,1)S(1)} %get-tuple-element.30.c_ref.wide), custom_call_target="tpu_custom_call" | custom-call | flops 4000000000 | bytes 2000000 | tf_op jit(solution)/shard_map/sent_sums/pallas_call | solution.py:220
  13.6 1.3 %collective-permute-start = (bf16[272,256]{1,0:T(8,128)(2,1)S(1)}, bf16[272,256]{1,0:T(8,128)(2,1)S(1)}, u32[]{:S(2)}, u32[]{:S(2)}) collective-permute-start(bf16[272,256]{1,0:T(8,128)(2,1)S(1)} %get-tuple-element.31), channel_id=1, source_target_pairs={{0,64},{64,128},{128,192},{192,0},{1,65},{65,129},{129,193},{193,1... | collective-permute-start | bytes 417800 | tf_op jit(solution)/shard_map/ppermute | solution.py:319
  14.9 3.2 %sent_sums.5 = (bf16[528,256]{1,0:T(8,128)(2,1)S(1)}, bf16[528,256]{1,0:T(8,128)(2,1)S(1)}, bf16[64,32,1024]{2,1,0:T(8,128)(2,1)S(1)}) custom-call(bf16[64,64,1024]{2,1,0:T(8,128)(2,1)} %x_ref.5, bf16[256,512]{1,0:T(8,128)(2,1)S(1)} %get-tuple-element.30.c_ref.wide), custom_call_target="tpu_custom_call" | custom-call | flops 4000000000 | bytes 2000000 | tf_op jit(solution)/shard_map/sent_sums/pallas_call | solution.py:220
  18.1 0.1 collective-permute-start.4
  18.2 3.6 %collective-permute-start.5 = (bf16[528,256]{1,0:T(8,128)(2,1)S(1)}, bf16[528,256]{1,0:T(8,128)(2,1)S(1)}, u32[]{:S(2)}, u32[]{:S(2)}) collective-permute-start(bf16[528,256]{1,0:T(8,128)(2,1)S(1)} %get-tuple-element.43), channel_id=1, source_target_pairs={{0,192},{64,0},{128,64},{192,128},{1,193},{65,1},{129,65},{193,129... | collective-permute-start | bytes 811016 | tf_op jit(solution)/shard_map/ppermute | solution.py:320
  21.8 1.5 %kept_sums.1 = (f32[16,64,256]{2,1,0:T(8,128)S(1)}, f32[16,64,128]{2,1,0:T(8,128)S(1)}, f32[16,64,128]{2,1,0:T(8,128)S(1)}) custom-call(bf16[256,512]{1,0:T(8,128)(2,1)S(1)} %get-tuple-element.30.c_ref.wide, bf16[64,16,1024]{2,1,0:T(8,128)(2,1)S(1)} %get-tuple-element.33.refs_0_, bf16[64,32,1024]{2,1,0:T(8,128)(2,1)S(1)} %get-tuple-element.34.refs_1_, ...), custom_call_target="tpu_custom_call" | custom-call | flops 6000000000 | bytes 2000000 | tf_op jit(solution)/shard_map/kept_sums/pallas_call | solution.py:242
  23.3 0.0 collective-permute-done.8.prev_ref
  23.3 1.2 %collective-permute-start.1 = (bf16[272,256]{1,0:T(8,128)(2,1)S(1)}, bf16[272,256]{1,0:T(8,128)(2,1)S(1)}, u32[]{:S(2)}, u32[]{:S(2)}) collective-permute-start(bf16[272,256]{1,0:T(8,128)(2,1)S(1)} %get-tuple-element.32), channel_id=1, source_target_pairs={{0,192},{64,0},{128,64},{192,128},{1,193},{65,1},{129,65},{193,129... | collective-permute-start | bytes 417800 | tf_op jit(solution)/shard_map/ppermute | solution.py:320
  24.6 0.0 collective-permute-done.9.next_ref
  24.6 0.4 relay.5
  24.9 1.3 %collective-permute-start.10 = (bf16[272,128]{1,0:T(8,128)(2,1)S(1)}, bf16[272,128]{1,0:T(8,128)(2,1)S(1)}, u32[]{:S(2)}, u32[]{:S(2)}) collective-permute-start(bf16[272,128]{1,0:T(8,128)(2,1)S(1)} %get-tuple-element.49), channel_id=1, source_target_pairs={{0,64},{64,128},{128,192},{192,0},{1,65},{65,129},{129,193},{193,1... | collective-permute-start | bytes 208904 | tf_op jit(solution)/shard_map/ppermute | solution.py:319
  26.2 10.9 %collective-permute-done.4.prev_ref = bf16[528,256]{1,0:T(8,128)(2,1)S(1)} collective-permute-done((bf16[528,256]{1,0:T(8,128)(2,1)S(1)}, bf16[528,256]{1,0:T(8,128)(2,1)S(1)}, u32[]{:S(2)}, u32[]{:S(2)}) %collective-permute-start.4) | collective-permute-done | bytes 270368 | tf_op jit(solution)/shard_map/ppermute | solution.py:319
  37.2 1.4 %collective-permute-start.11 = (bf16[272,128]{1,0:T(8,128)(2,1)S(1)}, bf16[272,128]{1,0:T(8,128)(2,1)S(1)}, u32[]{:S(2)}, u32[]{:S(2)}) collective-permute-start(bf16[272,128]{1,0:T(8,128)(2,1)S(1)} %get-tuple-element.50), channel_id=1, source_target_pairs={{0,192},{64,0},{128,64},{192,128},{1,193},{65,1},{129,65},{193,129... | collective-permute-start | bytes 208904 | tf_op jit(solution)/shard_map/ppermute | solution.py:320
  38.6 0.0 collective-permute-done.5.next_ref
  38.6 0.6 relay.4
  39.2 1.0 %collective-permute-start.6 = (bf16[528,128]{1,0:T(8,128)(2,1)S(1)}, bf16[528,128]{1,0:T(8,128)(2,1)S(1)}, u32[]{:S(2)}, u32[]{:S(2)}) collective-permute-start(bf16[528,128]{1,0:T(8,128)(2,1)S(1)} %get-tuple-element.44), channel_id=1, source_target_pairs={{0,64},{64,128},{128,192},{192,0},{1,65},{65,129},{129,193},{193,1... | collective-permute-start | bytes 405512 | tf_op jit(solution)/shard_map/ppermute | solution.py:319
  40.2 2.7 %collective-permute-start.7 = (bf16[528,128]{1,0:T(8,128)(2,1)S(1)}, bf16[528,128]{1,0:T(8,128)(2,1)S(1)}, u32[]{:S(2)}, u32[]{:S(2)}) collective-permute-start(bf16[528,128]{1,0:T(8,128)(2,1)S(1)} %get-tuple-element.45), channel_id=1, source_target_pairs={{0,192},{64,0},{128,64},{192,128},{1,193},{65,1},{129,65},{193,129... | collective-permute-start | bytes 405512 | tf_op jit(solution)/shard_map/ppermute | solution.py:320
  42.9 0.3 relay.3
  43.2 0.9 %collective-permute-start.2 = (bf16[272,128]{1,0:T(8,128)(2,1)S(1)}, bf16[272,128]{1,0:T(8,128)(2,1)S(1)}, u32[]{:S(2)}, u32[]{:S(2)}) collective-permute-start(bf16[272,128]{1,0:T(8,128)(2,1)S(1)} %get-tuple-element.39), channel_id=1, source_target_pairs={{0,64},{64,128},{128,192},{192,0},{1,65},{65,129},{129,193},{193,1... | collective-permute-start | bytes 208904 | tf_op jit(solution)/shard_map/ppermute | solution.py:319
  44.1 0.0 collective-permute-done.10.prev_ref
  44.1 2.8 %collective-permute-start.3 = (bf16[272,128]{1,0:T(8,128)(2,1)S(1)}, bf16[272,128]{1,0:T(8,128)(2,1)S(1)}, u32[]{:S(2)}, u32[]{:S(2)}) collective-permute-start(bf16[272,128]{1,0:T(8,128)(2,1)S(1)} %get-tuple-element.40), channel_id=1, source_target_pairs={{0,192},{64,0},{128,64},{192,128},{1,193},{65,1},{129,65},{193,129... | collective-permute-start | bytes 208904 | tf_op jit(solution)/shard_map/ppermute | solution.py:320
  46.9 0.8 %finish.3 = (f32[16,64,256]{2,1,0:T(8,128)}, f32[16,128]{1,0:T(8,128)S(1)}) custom-call(bf16[272,128]{1,0:T(8,128)(2,1)S(1)} %collective-permute-done.10.prev_ref, bf16[272,128]{1,0:T(8,128)(2,1)S(1)} %collective-permute-done.11.next_ref, f32[16,16,256]{2,1,0:T(8,128)S(1)} %get-tuple-element.51.sum_ref), custom_call_target="tpu_custom_call" | custom-call | flops 1000000000 | bytes 2000000 | tf_op jit(solution)/shard_map/finish/pallas_call | solution.py:284
  47.8 1.2 %collective-permute-done.7.next_ref = bf16[528,128]{1,0:T(8,128)(2,1)S(1)} collective-permute-done((bf16[528,128]{1,0:T(8,128)(2,1)S(1)}, bf16[528,128]{1,0:T(8,128)(2,1)S(1)}, u32[]{:S(2)}, u32[]{:S(2)}) %collective-permute-start.7) | collective-permute-done | bytes 135200 | tf_op jit(solution)/shard_map/ppermute | solution.py:320
  49.0 1.0 %finish.4 = (f32[16,64,256]{2,1,0:T(8,128)}, f32[16,128]{1,0:T(8,128)S(1)}) custom-call(bf16[528,128]{1,0:T(8,128)(2,1)S(1)} %collective-permute-done.6.prev_ref, bf16[528,128]{1,0:T(8,128)(2,1)S(1)} %collective-permute-done.7.next_ref, f32[16,32,256]{2,1,0:T(8,128)S(1)} %get-tuple-element.46.sum_ref, ...), custom_call_target="tpu_custom_call", output_to_operand_aliasing={{0}: (4, {})} | custom-call | flops 1000000000 | bytes 2000000 | tf_op jit(solution)/shard_map/finish/pallas_call | solution.py:284
  50.0 0.4 collective-permute-done.3.next_ref
  50.5 0.8 %finish.5 = (f32[16,64,256]{2,1,0:T(8,128)}, f32[256,16]{1,0:T(8,128)S(1)}) custom-call(bf16[272,128]{1,0:T(8,128)(2,1)S(1)} %collective-permute-done.2.prev_ref, bf16[272,128]{1,0:T(8,128)(2,1)S(1)} %collective-permute-done.3.next_ref, f32[16,16,256]{2,1,0:T(8,128)S(1)} %get-tuple-element.41.sum_ref, ...), custom_call_target="tpu_custom_call", output_to_operand_aliasing={{0}: (4, {})} | custom-call | flops 1000000000 | bytes 2000000 | tf_op jit(solution)/shard_map/finish/pallas_call | solution.py:284
  51.3 26.0 %all_to_all.9 = f32[256,1,16]{2,1,0:T(1,128)S(1)} all-to-all(f32[256,1,16]{2,1,0:T(1,128)S(1)} %bitcast.3), channel_id=1, replica_groups=mesh['snap'=4,'param'=64] {'snap','param'}, dimensions={0} | all-to-all | bytes 32768 | tf_op jit(solution)/shard_map/all_to_all | solution.py:338
  77.4 0.3 reduce_sum.9
  77.6 0.5 multiply_sqrt_fusion
  (5 shorter events, 0.0 us)
Async XLA Ops:
  3.1 20.2 %collective-permute-start.8 = (bf16[272,256]{1,0:T(8,128)(2,1)S(1)}, bf16[272,256]{1,0:T(8,128)(2,1)S(1)}, u32[]{:S(2)}, u32[]{:S(2)}) collective-permute-start(bf16[272,256]{1,0:T(8,128)(2,1)S(1)} %get-tuple-element.47), channel_id=1, source_target_pairs={{0,64},{64,0},{128,192},{192,128},{1,65},{65,1},{129,193},{193,129... | collective-permute-start | bytes 417800 | tf_op jit(solution)/shard_map/ppermute | solution.py:319
  7.0 17.6 %collective-permute-start.9 = (bf16[272,256]{1,0:T(8,128)(2,1)S(1)}, bf16[272,256]{1,0:T(8,128)(2,1)S(1)}, u32[]{:S(2)}, u32[]{:S(2)}) collective-permute-start(bf16[272,256]{1,0:T(8,128)(2,1)S(1)} %get-tuple-element.48), channel_id=1, source_target_pairs={{0,192},{64,128},{128,64},{192,0},{1,193},{65,129},{129,65},{193,1... | collective-permute-start | bytes 417800 | tf_op jit(solution)/shard_map/ppermute | solution.py:320
  13.6 26.6 %collective-permute-start = (bf16[272,256]{1,0:T(8,128)(2,1)S(1)}, bf16[272,256]{1,0:T(8,128)(2,1)S(1)}, u32[]{:S(2)}, u32[]{:S(2)}) collective-permute-start(bf16[272,256]{1,0:T(8,128)(2,1)S(1)} %get-tuple-element.31), channel_id=1, source_target_pairs={{0,64},{64,128},{128,192},{192,0},{1,65},{65,129},{129,193},{193,1... | collective-permute-start | bytes 417800 | tf_op jit(solution)/shard_map/ppermute | solution.py:319
  18.1 19.0 %collective-permute-start.4 = (bf16[528,256]{1,0:T(8,128)(2,1)S(1)}, bf16[528,256]{1,0:T(8,128)(2,1)S(1)}, u32[]{:S(2)}, u32[]{:S(2)}) collective-permute-start(bf16[528,256]{1,0:T(8,128)(2,1)S(1)} %get-tuple-element.42), channel_id=1, source_target_pairs={{0,64},{64,128},{128,192},{192,0},{1,65},{65,129},{129,193},{193,1... | collective-permute-start | bytes 811016 | tf_op jit(solution)/shard_map/ppermute | solution.py:319
  18.2 20.4 %collective-permute-start.5 = (bf16[528,256]{1,0:T(8,128)(2,1)S(1)}, bf16[528,256]{1,0:T(8,128)(2,1)S(1)}, u32[]{:S(2)}, u32[]{:S(2)}) collective-permute-start(bf16[528,256]{1,0:T(8,128)(2,1)S(1)} %get-tuple-element.43), channel_id=1, source_target_pairs={{0,192},{64,0},{128,64},{192,128},{1,193},{65,1},{129,65},{193,129... | collective-permute-start | bytes 811016 | tf_op jit(solution)/shard_map/ppermute | solution.py:320
  23.3 19.6 %collective-permute-start.1 = (bf16[272,256]{1,0:T(8,128)(2,1)S(1)}, bf16[272,256]{1,0:T(8,128)(2,1)S(1)}, u32[]{:S(2)}, u32[]{:S(2)}) collective-permute-start(bf16[272,256]{1,0:T(8,128)(2,1)S(1)} %get-tuple-element.32), channel_id=1, source_target_pairs={{0,192},{64,0},{128,64},{192,128},{1,193},{65,1},{129,65},{193,129... | collective-permute-start | bytes 417800 | tf_op jit(solution)/shard_map/ppermute | solution.py:320
  24.9 19.2 %collective-permute-start.10 = (bf16[272,128]{1,0:T(8,128)(2,1)S(1)}, bf16[272,128]{1,0:T(8,128)(2,1)S(1)}, u32[]{:S(2)}, u32[]{:S(2)}) collective-permute-start(bf16[272,128]{1,0:T(8,128)(2,1)S(1)} %get-tuple-element.49), channel_id=1, source_target_pairs={{0,64},{64,128},{128,192},{192,0},{1,65},{65,129},{129,193},{193,1... | collective-permute-start | bytes 208904 | tf_op jit(solution)/shard_map/ppermute | solution.py:319
  37.2 9.7 %collective-permute-start.11 = (bf16[272,128]{1,0:T(8,128)(2,1)S(1)}, bf16[272,128]{1,0:T(8,128)(2,1)S(1)}, u32[]{:S(2)}, u32[]{:S(2)}) collective-permute-start(bf16[272,128]{1,0:T(8,128)(2,1)S(1)} %get-tuple-element.50), channel_id=1, source_target_pairs={{0,192},{64,0},{128,64},{192,128},{1,193},{65,1},{129,65},{193,129... | collective-permute-start | bytes 208904 | tf_op jit(solution)/shard_map/ppermute | solution.py:320
  39.2 8.5 %collective-permute-start.6 = (bf16[528,128]{1,0:T(8,128)(2,1)S(1)}, bf16[528,128]{1,0:T(8,128)(2,1)S(1)}, u32[]{:S(2)}, u32[]{:S(2)}) collective-permute-start(bf16[528,128]{1,0:T(8,128)(2,1)S(1)} %get-tuple-element.44), channel_id=1, source_target_pairs={{0,64},{64,128},{128,192},{192,0},{1,65},{65,129},{129,193},{193,1... | collective-permute-start | bytes 405512 | tf_op jit(solution)/shard_map/ppermute | solution.py:319
  40.2 8.8 %collective-permute-start.7 = (bf16[528,128]{1,0:T(8,128)(2,1)S(1)}, bf16[528,128]{1,0:T(8,128)(2,1)S(1)}, u32[]{:S(2)}, u32[]{:S(2)}) collective-permute-start(bf16[528,128]{1,0:T(8,128)(2,1)S(1)} %get-tuple-element.45), channel_id=1, source_target_pairs={{0,192},{64,0},{128,64},{192,128},{1,193},{65,1},{129,65},{193,129... | collective-permute-start | bytes 405512 | tf_op jit(solution)/shard_map/ppermute | solution.py:320
  43.2 6.8 %collective-permute-start.2 = (bf16[272,128]{1,0:T(8,128)(2,1)S(1)}, bf16[272,128]{1,0:T(8,128)(2,1)S(1)}, u32[]{:S(2)}, u32[]{:S(2)}) collective-permute-start(bf16[272,128]{1,0:T(8,128)(2,1)S(1)} %get-tuple-element.39), channel_id=1, source_target_pairs={{0,64},{64,128},{128,192},{192,0},{1,65},{65,129},{129,193},{193,1... | collective-permute-start | bytes 208904 | tf_op jit(solution)/shard_map/ppermute | solution.py:319
  44.1 6.3 %collective-permute-start.3 = (bf16[272,128]{1,0:T(8,128)(2,1)S(1)}, bf16[272,128]{1,0:T(8,128)(2,1)S(1)}, u32[]{:S(2)}, u32[]{:S(2)}) collective-permute-start(bf16[272,128]{1,0:T(8,128)(2,1)S(1)} %get-tuple-element.40), channel_id=1, source_target_pairs={{0,192},{64,0},{128,64},{192,128},{1,193},{65,1},{129,65},{193,129... | collective-permute-start | bytes 208904 | tf_op jit(solution)/shard_map/ppermute | solution.py:320
